TPU v7x, 64 devices: a 2x2x8 block of a 4x4x8 slice. The times are simulated.
64 devices in a mesh: dp: 4 (over x, y), sp: 16 (over z, core).
Axes of the slice: x: 2, y: 2, z: 8, core: 2. Of those that a mesh axis runs over, the one named last changes fastest.
The devices are a block of a 4x4x8 slice.
Arguments:
- images: bfloat16 [128, 32, 256, 128], P('dp', 'sp'), parts along dimension 0
- w_a: bfloat16 [2, 3, 3, 128, 128], replicated
- bn_a: float32 [2, 2, 128], replicated
- w_down: bfloat16 [3, 3, 128, 1024], replicated
- bn_down: float32 [2, 1024], replicated
- w_in: bfloat16 [3, 1024, 256], replicated
- bn_in: float32 [3, 2, 256], replicated
- w_mid: bfloat16 [3, 3, 3, 256, 256], replicated
- bn_mid: float32 [3, 2, 256], replicated
- w_out: bfloat16 [3, 256, 1024], replicated
- bn_out: float32 [3, 2, 1024], replicated
Outputs:
- output: bfloat16 [128, 16, 128, 1024], P('dp', 'sp'), parts along dimension 0
There are 4 independent parts. A program takes and returns all parts, laid end to end along the dimension named above; an argument that names none is the same for every part.
All inputs are finite; a program needn't handle non-finite values.
Results may differ from a plain program's by a relative error of at most 0.02.
Values are sent between devices in bfloat16 or wider.
A program may use at most 768 MiB of HBM per device.

v0:
```python
import jax
import jax.numpy as jnp
from jax import lax
from jax.sharding import PartitionSpec as P, NamedSharding

NORM_EPS = 1e-5
CONV_DIMS = ("NHWC", "HWIO", "NHWC")


def solution(mesh):
    groups = mesh.shape["sp"]
    to_next = [(device, device + 1) for device in range(groups - 1)]
    to_prev = [(device + 1, device) for device in range(groups - 1)]

    def conv_same(hidden, weight):
        from_above = lax.ppermute(hidden[:, -1:], "sp", to_next)
        from_below = lax.ppermute(hidden[:, :1], "sp", to_prev)
        padded = jnp.concatenate([from_above, hidden, from_below], axis=1)
        return lax.conv_general_dilated(padded, weight, (1, 1), ((0, 0), (1, 1)), dimension_numbers=CONV_DIMS, preferred_element_type=jnp.float32)

    def conv_down(hidden, weight):
        from_below = lax.ppermute(hidden[:, :1], "sp", to_prev)
        padded = jnp.concatenate([hidden, from_below], axis=1)
        return lax.conv_general_dilated(padded, weight, (2, 2), ((0, 0), (0, 1)), dimension_numbers=CONV_DIMS, preferred_element_type=jnp.float32)

    def conv_point(hidden, weight):
        return jnp.einsum("bhwc,cd->bhwd", hidden, weight, preferred_element_type=jnp.float32)

    def batch_norm(pre_act, params):
        norm_count = pre_act.shape[0] * pre_act.shape[1] * pre_act.shape[2] * groups
        part_sums = jnp.stack([jnp.sum(pre_act, axis=(0, 1, 2)), jnp.sum(pre_act * pre_act, axis=(0, 1, 2))])
        group_moments = lax.psum(part_sums, "sp") / norm_count
        chan_mean = group_moments[0]
        chan_var = group_moments[1] - chan_mean * chan_mean
        chan_scale = params[0] * lax.rsqrt(chan_var + NORM_EPS)
        return (pre_act - chan_mean) * chan_scale + params[1]

    def norm_relu(pre_act, params):
        return jax.nn.relu(batch_norm(pre_act, params)).astype(jnp.bfloat16)

    def forward(images, w_a, bn_a, w_down, bn_down, w_in, bn_in, w_mid, bn_mid, w_out, bn_out):
        hidden = images
        for layer_num in range(w_a.shape[0]):
            hidden = norm_relu(conv_same(hidden, w_a[layer_num]), bn_a[layer_num])
        hidden = norm_relu(conv_down(hidden, w_down), bn_down)
        for block_num in range(w_in.shape[0]):
            branch = norm_relu(conv_point(hidden, w_in[block_num]), bn_in[block_num])
            branch = norm_relu(conv_same(branch, w_mid[block_num]), bn_mid[block_num])
            summed = batch_norm(conv_point(branch, w_out[block_num]), bn_out[block_num]) + hidden
            hidden = jax.nn.relu(summed).astype(jnp.bfloat16)
        return hidden

    act_spec = P("dp", "sp", None, None)
    return jax.shard_map(forward, mesh=mesh, in_specs=(act_spec,) + (P(),) * 10, out_specs=act_spec, check_vma=False)
```

profile of v0, /device:TPU:21, one launch (start us, length us, event | category | flops | bytes accessed | tf_op | source)
XLA Modules:
  0.0 714.6 jit_solution(4431799364948464002)
XLA Ops:
  13.9 20.0 %collective-permute-done = bf16[32,1,256,128]{3,0,2,1:T(8,128)(2,1)S(1)} collective-permute-done((bf16[32,1,256,128]{3,0,2,1:T(8,128)(2,1)S(1)}, bf16[32,1,256,128]{3,0,2,1:T(8,128)(2,1)S(1)}, u32[]{:S(2)}, u32[]{:S(2)}) %collective-permute-start) | collective-permute-done | bytes 2097184 | tf_op jit(solution)/shard_map/ppermute | solution.py:16
  50.7 25.5 %psum.84 = f32[2,128]{1,0:T(2,128)S(1)} all-reduce(f32[2,128]{1,0:T(2,128)S(1)} %pad_maximum_fusion.13), channel_id=1, replica_groups=mesh['dp'=4,'sp'=16] {'sp'}, use_global_device_ids=true, to_apply=%region_2.0 | all-reduce | flops 256 | bytes 2048 | tf_op jit(solution)/shard_map/psum | solution.py:32
  87.3 19.4 %collective-permute-done.2 = bf16[32,1,256,128]{3,0,2,1:T(8,128)(2,1)S(1)} collective-permute-done((bf16[32,1,256,128]{3,0,2,1:T(8,128)(2,1)S(1)}, bf16[32,1,256,128]{3,0,2,1:T(8,128)(2,1)S(1)}, u32[]{:S(2)}, u32[]{:S(2)}) %collective-permute-start.2) | collective-permute-done | bytes 2097184 | tf_op jit(solution)/shard_map/ppermute | solution.py:16
  123.8 24.0 %psum.85 = f32[2,128]{1,0:T(2,128)S(1)} all-reduce(f32[2,128]{1,0:T(2,128)S(1)} %pad_maximum_fusion.14), channel_id=1, replica_groups=mesh['dp'=4,'sp'=16] {'sp'}, use_global_device_ids=true, to_apply=%region_5.6 | all-reduce | flops 256 | bytes 2048 | tf_op jit(solution)/shard_map/psum | solution.py:32
  155.9 25.1 %collective-permute-done.4 = bf16[32,1,256,128]{3,0,2,1:T(8,128)(2,1)S(1)} collective-permute-done((bf16[32,1,256,128]{3,0,2,1:T(8,128)(2,1)S(1)}, bf16[32,1,256,128]{3,0,2,1:T(8,128)(2,1)S(1)}, u32[]{:S(2)}, u32[]{:S(2)}) %collective-permute-start.4) | collective-permute-done | bytes 2097184 | tf_op jit(solution)/shard_map/ppermute | solution.py:22
  181.0 13.5 %fusion.87 = (f32[1024]{0:T(1024)S(1)}, f32[1024]{0:T(1024)S(1)}, f32[32,1,128,1024]{3,0,2,1:T(8,128)}) fusion(bf16[3,3,128,1024]{3,2,1,0:T(8,128)(2,1)S(1)} %copy-done, bf16[32,1,256,128]{3,0,2,1:T(8,128)(2,1)S(1)} %collective-permute-done.4, bf16[32,2,256,128]{3,0,2,1:T(8,128)(2,1)S(1)} %maximum_convert_fusion.1), kind=kOutput, calls=%fused_computation.157 | convolution fusion | flops 9663674368 | bytes 25436160 | tf_op jit(solution)/shard_map/conv_general_dilated | solution.py:24
  194.5 25.0 %psum.86 = f32[2,1024]{1,0:T(2,128)S(1)} all-reduce(f32[2,1024]{1,0:T(2,128)S(1)} %pad_maximum_fusion.3), channel_id=1, replica_groups=mesh['dp'=4,'sp'=16] {'sp'}, use_global_device_ids=true, to_apply=%region_8.9 | all-reduce | flops 2048 | bytes 16384 | tf_op jit(solution)/shard_map/psum | solution.py:32
  239.8 23.8 %psum.87 = f32[2,256]{1,0:T(2,128)S(1)} all-reduce(f32[2,256]{1,0:T(2,128)S(1)} %pad_maximum_fusion.7), channel_id=1, replica_groups=mesh['dp'=4,'sp'=16] {'sp'}, use_global_device_ids=true, to_apply=%region_11.12 | all-reduce | flops 512 | bytes 4096 | tf_op jit(solution)/shard_map/psum | solution.py:32
  273.2 21.5 %collective-permute-done.6 = bf16[32,1,128,256]{3,2,0,1:T(8,128)(2,1)S(1)} collective-permute-done((bf16[32,1,128,256]{3,2,0,1:T(8,128)(2,1)S(1)}, bf16[32,1,128,256]{3,2,0,1:T(8,128)(2,1)S(1)}, u32[]{:S(2)}, u32[]{:S(2)}) %collective-permute-start.6) | collective-permute-done | bytes 2097184 | tf_op jit(solution)/shard_map/ppermute | solution.py:17
  305.9 26.4 %psum.88 = f32[2,256]{1,0:T(2,128)S(1)} all-reduce(f32[2,256]{1,0:T(2,128)S(1)} %pad_maximum_fusion.8), channel_id=1, replica_groups=mesh['dp'=4,'sp'=16] {'sp'}, use_global_device_ids=true, to_apply=%region_14.15 | all-reduce | flops 512 | bytes 4096 | tf_op jit(solution)/shard_map/psum | solution.py:32
  343.7 23.6 %psum.89 = f32[2,1024]{1,0:T(2,128)S(1)} all-reduce(f32[2,1024]{1,0:T(2,128)S(1)} %pad_maximum_fusion.4), channel_id=1, replica_groups=mesh['dp'=4,'sp'=16] {'sp'}, use_global_device_ids=true, to_apply=%region_17.18 | all-reduce | flops 2048 | bytes 16384 | tf_op jit(solution)/shard_map/psum | solution.py:32
  367.3 19.3 %fusion.5 = bf16[32,1,128,1024]{3,0,2,1:T(8,128)(2,1)S(1)} fusion(f32[32,128,1024]{2,1,0:T(8,128)} %get-tuple-element.80, f32[1024]{0:T(1024)S(1)} %bitcast.221, f32[1024]{0:T(1024)S(1)} %rsqrt_multiply_fusion.2, f32[1024]{0:T(1024)S(1)} %bitcast.204, f32[1024]{0:T(1024)S(1)} %bitcast.202, f32[1024]{0:T(1024)S(1)} %rsqrt_multiply_fusion.3, ...), kind=kLoop, calls=%fused_computation.8 | loop fusion | flops 50331648 | bytes 41967616 | tf_op jit(solution)/shard_map/convert_element_type | solution.py:50
  386.6 13.3 %fusion.93 = (f32[256]{0:T(256)S(1)}, f32[256]{0:T(256)S(1)}, f32[32,128,256]{2,1,0:T(8,128)}) fusion(bf16[3,1024,256]{2,1,0:T(8,128)(2,1)} %param.16, bf16[32,128,1024]{2,0,1:T(8,128)(2,1)S(1)} %bitcast.193), kind=kOutput, calls=%fused_computation.163 | convolution fusion | flops 2150628864 | bytes 13109248 | tf_op jit(solution)/shard_map/bhwc,cd->bhwd/dot_general | solution.py:27
  400.0 24.7 %psum.90 = f32[2,256]{1,0:T(2,128)S(1)} all-reduce(f32[2,256]{1,0:T(2,128)S(1)} %pad_maximum_fusion.9), channel_id=1, replica_groups=mesh['dp'=4,'sp'=16] {'sp'}, use_global_device_ids=true, to_apply=%region_20.21 | all-reduce | flops 512 | bytes 4096 | tf_op jit(solution)/shard_map/psum | solution.py:32
  433.3 21.7 %collective-permute-done.8 = bf16[32,1,128,256]{3,2,0,1:T(8,128)(2,1)S(1)} collective-permute-done((bf16[32,1,128,256]{3,2,0,1:T(8,128)(2,1)S(1)}, bf16[32,1,128,256]{3,2,0,1:T(8,128)(2,1)S(1)}, u32[]{:S(2)}, u32[]{:S(2)}) %collective-permute-start.8) | collective-permute-done | bytes 2097184 | tf_op jit(solution)/shard_map/ppermute | solution.py:17
  466.4 25.1 %psum.91 = f32[2,256]{1,0:T(2,128)S(1)} all-reduce(f32[2,256]{1,0:T(2,128)S(1)} %pad_maximum_fusion.10), channel_id=1, replica_groups=mesh['dp'=4,'sp'=16] {'sp'}, use_global_device_ids=true, to_apply=%region_23.24 | all-reduce | flops 512 | bytes 4096 | tf_op jit(solution)/shard_map/psum | solution.py:32
  502.9 23.6 %psum.92 = f32[2,1024]{1,0:T(2,128)S(1)} all-reduce(f32[2,1024]{1,0:T(2,128)S(1)} %pad_maximum_fusion.5), channel_id=1, replica_groups=mesh['dp'=4,'sp'=16] {'sp'}, use_global_device_ids=true, to_apply=%region_26.27 | all-reduce | flops 2048 | bytes 16384 | tf_op jit(solution)/shard_map/psum | solution.py:32
  526.6 17.7 %fusion.3 = bf16[32,1,128,1024]{3,0,2,1:T(8,128)(2,1)S(1)} fusion(f32[32,128,1024]{2,1,0:T(8,128)} %get-tuple-element.83, bf16[32,1,128,1024]{3,0,2,1:T(8,128)(2,1)} %copy-done.3, f32[1024]{0:T(1024)S(1)} %bitcast.206, f32[1024]{0:T(1024)S(1)} %rsqrt_multiply_fusion.1, f32[1024]{0:T(1024)S(1)} %bitcast.200), kind=kLoop, calls=%fused_computation.5 | loop fusion | flops 29360128 | bytes 33566720 | tf_op jit(solution)/shard_map/convert_element_type | solution.py:50
  544.2 13.2 %fusion.91 = (f32[256]{0:T(256)S(1)}, f32[256]{0:T(256)S(1)}, f32[32,128,256]{2,1,0:T(8,128)}) fusion(bf16[3,1024,256]{2,1,0:T(8,128)(2,1)} %param.16, bf16[32,128,1024]{2,0,1:T(8,128)(2,1)S(1)} %bitcast.192), kind=kOutput, calls=%fused_computation.161 | convolution fusion | flops 2150628864 | bytes 13109248 | tf_op jit(solution)/shard_map/bhwc,cd->bhwd/dot_general | solution.py:27
  557.4 24.7 %psum.93 = f32[2,256]{1,0:T(2,128)S(1)} all-reduce(f32[2,256]{1,0:T(2,128)S(1)} %pad_maximum_fusion.11), channel_id=1, replica_groups=mesh['dp'=4,'sp'=16] {'sp'}, use_global_device_ids=true, to_apply=%region_29.30 | all-reduce | flops 512 | bytes 4096 | tf_op jit(solution)/shard_map/psum | solution.py:32
  590.7 21.7 %collective-permute-done.10 = bf16[32,1,128,256]{3,2,0,1:T(8,128)(2,1)S(1)} collective-permute-done((bf16[32,1,128,256]{3,2,0,1:T(8,128)(2,1)S(1)}, bf16[32,1,128,256]{3,2,0,1:T(8,128)(2,1)S(1)}, u32[]{:S(2)}, u32[]{:S(2)}) %collective-permute-start.10) | collective-permute-done | bytes 2097184 | tf_op jit(solution)/shard_map/ppermute | solution.py:17
  623.6 25.1 %psum.94 = f32[2,256]{1,0:T(2,128)S(1)} all-reduce(f32[2,256]{1,0:T(2,128)S(1)} %pad_maximum_fusion.12), channel_id=1, replica_groups=mesh['dp'=4,'sp'=16] {'sp'}, use_global_device_ids=true, to_apply=%region_32.33 | all-reduce | flops 512 | bytes 4096 | tf_op jit(solution)/shard_map/psum | solution.py:32
  660.1 23.6 %psum.95 = f32[2,1024]{1,0:T(2,128)S(1)} all-reduce(f32[2,1024]{1,0:T(2,128)S(1)} %pad_maximum_fusion.6), channel_id=1, replica_groups=mesh['dp'=4,'sp'=16] {'sp'}, use_global_device_ids=true, to_apply=%region_35.36 | all-reduce | flops 2048 | bytes 16384 | tf_op jit(solution)/shard_map/psum | solution.py:32
  683.8 18.8 %fusion.1 = bf16[32,1,128,1024]{3,0,2,1:T(8,128)(2,1)} fusion(f32[32,128,1024]{2,1,0:T(8,128)} %get-tuple-element.86, bf16[32,1,128,1024]{3,0,2,1:T(8,128)(2,1)} %copy-done.2, f32[1024]{0:T(1024)S(1)} %bitcast.205, f32[1024]{0:T(1024)S(1)} %rsqrt_multiply_fusion, f32[1024]{0:T(1024)S(1)} %bitcast.198), kind=kLoop, calls=%fused_computation.2 | loop fusion | flops 29360128 | bytes 33566720 | tf_op jit(solution)/shard_map/convert_element_type | solution.py:50
  (115 shorter events, 193.5 us)
Async XLA Ops:
  0.0 181.0 %copy-start = (bf16[3,3,128,1024]{3,2,1,0:T(8,128)(2,1)S(1)}, bf16[3,3,128,1024]{3,2,1,0:T(8,128)(2,1)}, u32[]{:S(2)}) copy-start(bf16[3,3,128,1024]{3,2,1,0:T(8,128)(2,1)} %param.14) | copy-start | bytes 7077892
  5.0 8.8 %copy-start.8 = (f32[2,2,128]{2,1,0:T(2,128)S(1)}, f32[2,2,128]{2,1,0:T(2,128)}, u32[]{:S(2)}) copy-start(f32[2,2,128]{2,1,0:T(2,128)} %param.13) | copy-start | bytes 6148
  5.1 33.2 %copy-start.9 = (bf16[2,3,3,128,128]{4,3,2,1,0:T(8,128)(2,1)S(1)}, bf16[2,3,3,128,128]{4,3,2,1,0:T(8,128)(2,1)}, u32[]{:S(2)}) copy-start(bf16[2,3,3,128,128]{4,3,2,1,0:T(8,128)(2,1)} %param.12) | copy-start | bytes 1769476
  5.8 28.0 %collective-permute-start = (bf16[32,1,256,128]{3,0,2,1:T(8,128)(2,1)S(1)}, bf16[32,1,256,128]{3,0,2,1:T(8,128)(2,1)S(1)}, u32[]{:S(2)}, u32[]{:S(2)}) collective-permute-start(bf16[32,1,256,128]{3,0,2,1:T(8,128)(2,1)S(1)} %get-tuple-element.31), channel_id=1, source_target_pairs={{0,1},{1,2},{2,3},{3,4},{4,5},{5,6},{6,7},{7,8},{8,9},{9,10},{10,1... | collective-permute-start | bytes 6291464 | tf_op jit(solution)/shard_map/ppermute | solution.py:16
  10.9 27.4 %collective-permute-start.1 = (bf16[32,1,256,128]{3,0,2,1:T(8,128)(2,1)S(1)}, bf16[32,1,256,128]{3,0,2,1:T(8,128)(2,1)S(1)}, u32[]{:S(2)}, u32[]{:S(2)}) collective-permute-start(bf16[32,1,256,128]{3,0,2,1:T(8,128)(2,1)S(1)} %get-tuple-element.32), channel_id=1, source_target_pairs={{1,0},{2,1},{3,2},{4,3},{5,4},{6,5},{7,6},{8,7},{9,8},{10,9},{11,1... | collective-permute-start | bytes 6291464 | tf_op jit(solution)/shard_map/ppermute | solution.py:17
  81.7 25.0 %collective-permute-start.2 = (bf16[32,1,256,128]{3,0,2,1:T(8,128)(2,1)S(1)}, bf16[32,1,256,128]{3,0,2,1:T(8,128)(2,1)S(1)}, u32[]{:S(2)}, u32[]{:S(2)}) collective-permute-start(bf16[32,1,256,128]{3,0,2,1:T(8,128)(2,1)S(1)} %get-tuple-element.29), channel_id=1, source_target_pairs={{0,1},{1,2},{2,3},{3,4},{4,5},{5,6},{6,7},{7,8},{8,9},{9,10},{10,1... | collective-permute-start | bytes 6291464 | tf_op jit(solution)/shard_map/ppermute | solution.py:16
  84.0 27.4 %collective-permute-start.3 = (bf16[32,1,256,128]{3,0,2,1:T(8,128)(2,1)S(1)}, bf16[32,1,256,128]{3,0,2,1:T(8,128)(2,1)S(1)}, u32[]{:S(2)}, u32[]{:S(2)}) collective-permute-start(bf16[32,1,256,128]{3,0,2,1:T(8,128)(2,1)S(1)} %get-tuple-element.30), channel_id=1, source_target_pairs={{1,0},{2,1},{3,2},{4,3},{5,4},{6,5},{7,6},{8,7},{9,8},{10,9},{11,1... | collective-permute-start | bytes 6291464 | tf_op jit(solution)/shard_map/ppermute | solution.py:17
  152.6 3.2 copy-start.6
  152.7 3.2 copy-start.5
  153.0 27.9 %collective-permute-start.4 = (bf16[32,1,256,128]{3,0,2,1:T(8,128)(2,1)S(1)}, bf16[32,1,256,128]{3,0,2,1:T(8,128)(2,1)S(1)}, u32[]{:S(2)}, u32[]{:S(2)}) collective-permute-start(bf16[32,1,256,128]{3,0,2,1:T(8,128)(2,1)S(1)} %slice.315), channel_id=1, source_target_pairs={{1,0},{2,1},{3,2},{4,3},{5,4},{6,5},{7,6},{8,7},{9,8},{10,9},{11,1... | collective-permute-start | bytes 6291464 | tf_op jit(solution)/shard_map/ppermute | solution.py:22
  239.8 33.4 %copy-start.7 = (f32[3,2,256]{2,1,0:T(2,128)S(1)}, f32[3,2,256]{2,1,0:T(2,128)}, u32[]{:S(2)}) copy-start(f32[3,2,256]{2,1,0:T(2,128)} %param.19) | copy-start | bytes 18436
  239.8 33.4 %copy-start.4 = (f32[3,2,1024]{2,1,0:T(2,128)S(1)}, f32[3,2,1024]{2,1,0:T(2,128)}, u32[]{:S(2)}) copy-start(f32[3,2,1024]{2,1,0:T(2,128)} %param.21) | copy-start | bytes 73732
  266.5 28.3 %collective-permute-start.6 = (bf16[32,1,128,256]{3,2,0,1:T(8,128)(2,1)S(1)}, bf16[32,1,128,256]{3,2,0,1:T(8,128)(2,1)S(1)}, u32[]{:S(2)}, u32[]{:S(2)}) collective-permute-start(bf16[32,1,128,256]{3,2,0,1:T(8,128)(2,1)S(1)} %fusion.40), channel_id=1, source_target_pairs={{1,0},{2,1},{3,2},{4,3},{5,4},{6,5},{7,6},{8,7},{9,8},{10,9},{11,1... | collective-permute-start | bytes 6291464 | tf_op jit(solution)/shard_map/ppermute | solution.py:17
  269.3 26.8 %collective-permute-start.5 = (bf16[32,1,128,256]{3,2,0,1:T(8,128)(2,1)S(1)}, bf16[32,1,128,256]{3,2,0,1:T(8,128)(2,1)S(1)}, u32[]{:S(2)}, u32[]{:S(2)}) collective-permute-start(bf16[32,1,128,256]{3,2,0,1:T(8,128)(2,1)S(1)} %fusion.40), channel_id=1, source_target_pairs={{0,1},{1,2},{2,3},{3,4},{4,5},{5,6},{6,7},{7,8},{8,9},{9,10},{10,1... | collective-permute-start | bytes 6291464 | tf_op jit(solution)/shard_map/ppermute | solution.py:16
  386.6 13.4 %copy-start.3 = (bf16[32,1,128,1024]{3,0,2,1:T(8,128)(2,1)}, bf16[32,1,128,1024]{3,0,2,1:T(8,128)(2,1)S(1)}, u32[]{:S(2)}) copy-start(bf16[32,1,128,1024]{3,0,2,1:T(8,128)(2,1)S(1)} %fusion.5) | copy-start | bytes 25165828
  427.6 27.4 %collective-permute-start.8 = (bf16[32,1,128,256]{3,2,0,1:T(8,128)(2,1)S(1)}, bf16[32,1,128,256]{3,2,0,1:T(8,128)(2,1)S(1)}, u32[]{:S(2)}, u32[]{:S(2)}) collective-permute-start(bf16[32,1,128,256]{3,2,0,1:T(8,128)(2,1)S(1)} %fusion.42), channel_id=1, source_target_pairs={{1,0},{2,1},{3,2},{4,3},{5,4},{6,5},{7,6},{8,7},{9,8},{10,9},{11,1... | collective-permute-start | bytes 6291464 | tf_op jit(solution)/shard_map/ppermute | solution.py:17
  430.3 26.0 %collective-permute-start.7 = (bf16[32,1,128,256]{3,2,0,1:T(8,128)(2,1)S(1)}, bf16[32,1,128,256]{3,2,0,1:T(8,128)(2,1)S(1)}, u32[]{:S(2)}, u32[]{:S(2)}) collective-permute-start(bf16[32,1,128,256]{3,2,0,1:T(8,128)(2,1)S(1)} %fusion.42), channel_id=1, source_target_pairs={{0,1},{1,2},{2,3},{3,4},{4,5},{5,6},{6,7},{7,8},{8,9},{9,10},{10,1... | collective-permute-start | bytes 6291464 | tf_op jit(solution)/shard_map/ppermute | solution.py:16
  544.2 13.2 %copy-start.2 = (bf16[32,1,128,1024]{3,0,2,1:T(8,128)(2,1)}, bf16[32,1,128,1024]{3,0,2,1:T(8,128)(2,1)S(1)}, u32[]{:S(2)}) copy-start(bf16[32,1,128,1024]{3,0,2,1:T(8,128)(2,1)S(1)} %fusion.3) | copy-start | bytes 25165828
  585.0 27.4 %collective-permute-start.10 = (bf16[32,1,128,256]{3,2,0,1:T(8,128)(2,1)S(1)}, bf16[32,1,128,256]{3,2,0,1:T(8,128)(2,1)S(1)}, u32[]{:S(2)}, u32[]{:S(2)}) collective-permute-start(bf16[32,1,128,256]{3,2,0,1:T(8,128)(2,1)S(1)} %fusion.44), channel_id=1, source_target_pairs={{1,0},{2,1},{3,2},{4,3},{5,4},{6,5},{7,6},{8,7},{9,8},{10,9},{11,1... | collective-permute-start | bytes 6291464 | tf_op jit(solution)/shard_map/ppermute | solution.py:17
  587.7 26.0 %collective-permute-start.9 = (bf16[32,1,128,256]{3,2,0,1:T(8,128)(2,1)S(1)}, bf16[32,1,128,256]{3,2,0,1:T(8,128)(2,1)S(1)}, u32[]{:S(2)}, u32[]{:S(2)}) collective-permute-start(bf16[32,1,128,256]{3,2,0,1:T(8,128)(2,1)S(1)} %fusion.44), channel_id=1, source_target_pairs={{0,1},{1,2},{2,3},{3,4},{4,5},{5,6},{6,7},{7,8},{8,9},{9,10},{10,1... | collective-permute-start | bytes 6291464 | tf_op jit(solution)/shard_map/ppermute | solution.py:16
  702.5 11.6 %copy-start.1 = (bf16[3,3,128,1024]{3,2,1,0:T(8,128)(2,1)S(1)}, bf16[3,3,128,1024]{3,2,1,0:T(8,128)(2,1)}, u32[]{:S(2)}) copy-start(bf16[3,3,128,1024]{3,2,1,0:T(8,128)(2,1)} %param.14) | copy-start | bytes 7077892
where the time goes:
time: 726 us; the launch traced here: 715 us
  blocking collectives  295 us (41%)
  waiting for transfers between devices  142 us (20%)
  matrix products  130 us (18%)
  other arithmetic  93.5 us (13%)
  starting transfers between devices  34.3 us (5%)
  local copies, waits for them, and re-layouts  18.7 us (3%)
    psum x12, blocking collectives, batch_norm(): group_moments = lax.psum(part_sums, 'sp') / norm_count  295 us
    ppermute x5, waiting for transfers between devices, conv_same(): from_below = lax.ppermute(hidden[:, :1], 'sp', to_prev)  74.1 us
    dot_general x6, matrix products, conv_point(): jnp.einsum('bhwc,cd->bhwd', hidden, weight, preferred_element_type=jnp.fl...  64.8 us
    convert_element_type x3, other arithmetic, forward(): hidden = jax.nn.relu(summed).astype(jnp.bfloat16)  55.7 us
    conv_general_dilated x5, matrix products, conv_same(): lax.conv_general_dilated(padded, weight, (1, 1), ((0, 0), (1, 1)), dimens...  51.6 us
    ppermute x5, waiting for transfers between devices, conv_same(): from_above = lax.ppermute(hidden[:, -1:], 'sp', to_next)  43.1 us
    ppermute x1, waiting for transfers between devices, conv_down(): from_below = lax.ppermute(hidden[:, :1], 'sp', to_prev)  25.1 us
    convert_element_type x5, other arithmetic, norm_relu(): return jax.nn.relu(batch_norm(pre_act, params)).astype(jnp.bfloat16)  18.3 us
  transfers between devices with their start and end apart: 11, of which 11 were waited for; matrix products, arithmetic and copies ran while one was open for 0% of the time, Pallas kernels for 0%

commit v1 on v0

v1 whole, which is shorter than its diff:
```python
import jax
import jax.numpy as jnp
from jax import lax
from jax.experimental import pallas as pl
from jax.experimental.pallas import tpu as pltpu
from jax.sharding import PartitionSpec as P

NORM_EPS = 1e-5
CHUNKS = 8
TILE = 256
F32 = jnp.float32
BF16 = jnp.bfloat16


def solution(mesh):
    groups = mesh.shape["sp"]
    peers = sorted(range(1, groups), key=lambda k: (abs(2 * k - groups), k))

    def make_kernel(batch, rows, width, chan_a, chan_b, chan_m, layers, blocks):
        half_w = width // 2
        points = batch * half_w
        per_chunk = batch // CHUNKS
        half_b = batch // 2
        tiles = chan_b // TILE
        m_rows = points // CHUNKS
        count_a = float(batch * rows * width * groups)
        count_b = float(points * groups)
        ar_down = layers
        ar_in = ar_down + tiles
        ar_mid = ar_in + blocks
        ar_out = ar_mid + blocks
        ar_total = ar_out + blocks * tiles

        def kernel(images, w_a, w_down, w_in, w_mid, w_out, bn_a, bn_down, bn_in, bn_mid, bn_out, out,
                   xa, u, zb, h, u2, wa, wd, win, wmid, wout, st, nrm, tmp, arsend, arbuf,
                   sem_w, sem_img, a_send, a_recv, u_send, u_recv, ar_ssem, ar_rsem, sem_out):
            me = lax.axis_index("sp")
            has_prev = me > 0
            has_next = me < groups - 1
            prev = jnp.maximum(me - 1, 0)
            nxt = jnp.minimum(me + 1, groups - 1)

            def remote(src, dst, ssem, rsem, dev):
                return pltpu.make_async_remote_copy(src_ref=src, dst_ref=dst, send_sem=ssem, recv_sem=rsem,
                                                    device_id={"sp": dev}, device_id_type=pl.DeviceIdType.MESH)

            def img_copy(c, r):
                sl = pl.ds(c * per_chunk, per_chunk)
                return pltpu.make_async_copy(images.at[sl, r], xa.at[1 + r, sl], sem_img.at[r, c])

            def load_images(c, _):
                for r in range(2):
                    img_copy(c, r).start()
                return 0
            for dy in range(3):
                for dx in range(3):
                    for l in range(layers):
                        pltpu.make_async_copy(w_a.at[l, dy, dx], wa.at[l, pl.ds(dy * chan_a, chan_a), pl.ds(dx * chan_a, chan_a)], sem_w.at[0]).start()
            lax.fori_loop(0, CHUNKS, load_images, 0)

            barrier = pltpu.get_barrier_semaphore()
            for k in peers:
                pl.semaphore_signal(barrier, inc=1, device_id={"sp": lax.rem(me + k, groups)}, device_id_type=pl.DeviceIdType.MESH)
            pl.semaphore_wait(barrier, groups - 1)

            def a_copies(c, first):
                sl = pl.ds(c * per_chunk, per_chunk)
                top = images.at[sl, 0] if first else xa.at[1, sl]
                bot = images.at[sl, 1] if first else xa.at[2, sl]
                up = remote(top, xa.at[3, sl], a_send.at[0, c], a_recv.at[1, c], prev)
                down = remote(bot, xa.at[0, sl], a_send.at[1, c], a_recv.at[0, c], nxt)
                return up, down

            def d_copy(c):
                sl = pl.ds(c * per_chunk, per_chunk)
                return remote(u.at[0, sl], u.at[2, sl], u_send.at[0, c], u_recv.at[1, c], prev)

            def u_copies(c):
                sl = pl.ds(c * per_chunk, per_chunk)
                up = remote(u.at[1, sl], u.at[2, sl], u_send.at[0, c], u_recv.at[1, c], prev)
                down = remote(u.at[1, sl], u.at[0, sl], u_send.at[1, c], u_recv.at[0, c], nxt)
                return up, down

            def start_pair(up, down):
                @pl.when(has_prev)
                def _():
                    up.start()

                @pl.when(has_next)
                def _():
                    down.start()

            def wait_sends(pair_of):
                def body(c, _):
                    up, down = pair_of(c)

                    @pl.when(has_prev)
                    def _():
                        up.wait_send()

                    @pl.when(has_next)
                    def _():
                        down.wait_send()
                    return 0
                lax.fori_loop(0, CHUNKS, body, 0)

            def wait_halo(pair_of, c):
                up, down = pair_of(c)

                @pl.when(has_prev)
                def _():
                    down.wait_recv()

                @pl.when(has_next)
                def _():
                    up.wait_recv()

            def clear_moments():
                st[...] = jnp.zeros_like(st)

            def add_moments(z, lo):
                wide = z.shape[-1]
                z8 = z.reshape(z.shape[0] // 8, 8, wide)
                st[0, :, lo:lo + wide] += jnp.sum(z8, axis=0)
                st[1, :, lo:lo + wide] += jnp.sum(z8 * z8, axis=0)

            def ar_copy(a, k):
                return remote(arsend.at[a], arbuf.at[a, k - 1], ar_ssem.at[a], ar_rsem.at[a], lax.rem(me + k, groups))

            def send_moments(a, lo, wide):
                s = jnp.sum(st[0, :, lo:lo + wide], axis=0, keepdims=True)
                q = jnp.sum(st[1, :, lo:lo + wide], axis=0, keepdims=True)
                both = jnp.concatenate([s, q] * (TILE // wide), axis=1)
                arsend[a] = both
                for k in peers:
                    ar_copy(a, k).start()

            def recv_moments(a, params, lo, wide, count):
                pltpu.make_async_copy(arbuf.at[a], arbuf.at[a], ar_rsem.at[a]).wait()
                total = jnp.sum(arbuf[a], axis=0) + arsend[a]
                m = total[:, :wide] / count
                q = total[:, wide:2 * wide] / count
                v = q - m * m
                nrm[0:1, lo:lo + wide] = m
                nrm[1:2, lo:lo + wide] = params[0:1] * lax.rsqrt(v + NORM_EPS)
                nrm[2:3, lo:lo + wide] = params[1:2]
                pltpu.make_async_copy(arbuf.at[a], arbuf.at[a], ar_ssem.at[a]).wait()

            def norm(z, lo):
                wide = z.shape[-1]
                return (z - nrm[0:1, lo:lo + wide]) * nrm[1:2, lo:lo + wide] + nrm[2:3, lo:lo + wide]

            def norm_relu(z, lo):
                return jnp.maximum(norm(z, lo), 0.0)

            def from_left(y, wide):
                col = lax.broadcasted_iota(jnp.int32, y.shape, 0)
                return jnp.where(lax.rem(col, wide) == 0, 0.0, pltpu.roll(y, 1, 0))

            def from_right(y, wide):
                col = lax.broadcasted_iota(jnp.int32, y.shape, 0)
                return jnp.where(lax.rem(col, wide) == wide - 1, 0.0, pltpu.roll(y, y.shape[0] - 1, 0))

            def dot(x, w):
                return jnp.dot(x, w, preferred_element_type=F32)

            @pl.when(me == 0)
            def _():
                def body(b, _):
                    xa[0, b] = jnp.zeros((width, chan_a), BF16)
                    return 0
                lax.fori_loop(0, batch, body, 0)

            @pl.when(me == groups - 1)
            def _():
                def body(b, _):
                    xa[3, b] = jnp.zeros((width, chan_a), BF16)
                    u[2, b] = jnp.zeros((half_w, 2 * chan_a), BF16)
                    return 0
                lax.fori_loop(0, batch, body, 0)

            def send_a(c, _):
                start_pair(*a_copies(c, True))
                return 0
            lax.fori_loop(0, CHUNKS, send_a, 0)

            for dy in range(3):
                for dx in range(3):
                    row = (2 * dy + dx) * chan_a if dx < 2 else (6 + dy) * chan_a
                    pltpu.make_async_copy(w_down.at[dy, dx], wd.at[pl.ds(row, chan_a)], sem_w.at[1]).start()
                    for j in range(blocks):
                        pltpu.make_async_copy(w_mid.at[j, dy, dx], wmid.at[j, pl.ds(dy * chan_m, chan_m), pl.ds(dx * chan_m, chan_m)], sem_w.at[3]).start()
            pltpu.make_async_copy(w_in, win, sem_w.at[2]).start()
            pltpu.make_async_copy(w_out, wout, sem_w.at[4]).start()

            def wait_weight(ref, i):
                pltpu.make_async_copy(ref, ref, sem_w.at[i]).wait()

            wait_weight(wa, 0)

            def conv_a(l):
                clear_moments()
                for hb in range(2):
                    def body(i, _):
                        b = hb * half_b + i
                        c = b // per_chunk

                        @pl.when(lax.rem(b, per_chunk) == 0)
                        def _():
                            if l == 0:
                                for r in range(2):
                                    img_copy(c, r).wait()
                            wait_halo(lambda c: a_copies(c, l == 0), c)
                        for r in range(2):
                            x = jnp.concatenate([xa[r, b], xa[r + 1, b], xa[r + 2, b]], axis=1)
                            z = dot(x, wa[l, :, chan_a:2 * chan_a])
                            z = z + from_left(dot(x, wa[l, :, 0:chan_a]), width)
                            z = z + from_right(dot(x, wa[l, :, 2 * chan_a:3 * chan_a]), width)
                            lane = (2 * r + hb) * chan_a
                            zb[pl.ds(pl.multiple_of(i * width, width), width), lane:lane + chan_a] = z
                            add_moments(z, 0)
                        return 0
                    lax.fori_loop(0, half_b, body, 0)
                send_moments(l, 0, chan_a)
                wait_sends(lambda c: a_copies(c, l == 0))
                recv_moments(l, bn_a[l], 0, chan_a, count_a)

            conv_a(0)
            for l in range(1, layers):
                for hb in range(2):
                    def renorm(i, _):
                        b = hb * half_b + i
                        for r in range(2):
                            lane = (2 * r + hb) * chan_a
                            z = zb[pl.ds(pl.multiple_of(i * width, width), width), lane:lane + chan_a]
                            xa[1 + r, b] = norm_relu(z, 0).astype(BF16)

                        @pl.when(lax.rem(b, per_chunk) == per_chunk - 1)
                        def _():
                            start_pair(*a_copies(b // per_chunk, False))
                        return 0
                    lax.fori_loop(0, half_b, renorm, 0)
                conv_a(l)

            for hb in range(2):
                def pair_up(i, _):
                    b = hb * half_b + i
                    for r in range(2):
                        lane = (2 * r + hb) * chan_a
                        z = zb[pl.ds(pl.multiple_of(i * width, width), width), lane:lane + chan_a]
                        tmp[r] = norm_relu(z, 0)
                        u[r, b, :, 0:chan_a] = tmp[r, pl.ds(0, half_w, stride=2), :].astype(BF16)
                        u[r, b, :, chan_a:2 * chan_a] = tmp[r, pl.ds(1, half_w, stride=2), :].astype(BF16)

                    @pl.when(jnp.logical_and(lax.rem(b, per_chunk) == per_chunk - 1, has_prev))
                    def _():
                        d_copy(b // per_chunk).start()
                    return 0
                lax.fori_loop(0, half_b, pair_up, 0)

            wait_weight(wd, 1)
            clear_moments()

            def down_body(c, _):
                @pl.when(has_next)
                def _():
                    d_copy(c).wait_recv()
                sl = pl.ds(c * per_chunk, per_chunk)
                flat = [u[r, sl].reshape(m_rows, 2 * chan_a) for r in range(3)]
                evens = [from_right(f[:, :chan_a].astype(F32), half_w).astype(BF16) for f in flat]
                x = jnp.concatenate(flat + evens, axis=1)
                rows_at = pl.ds(pl.multiple_of(c * m_rows, m_rows), m_rows)
                for t in range(tiles):
                    z = dot(x, wd[:, t * TILE:(t + 1) * TILE])
                    zb[rows_at, t * TILE:(t + 1) * TILE] = z
                    add_moments(z, t * TILE)
                return 0
            lax.fori_loop(0, CHUNKS, down_body, 0)
            for t in range(tiles):
                send_moments(ar_down + t, t * TILE, TILE)

            def wait_d(c, _):
                @pl.when(has_prev)
                def _():
                    d_copy(c).wait_send()
                return 0
            lax.fori_loop(0, CHUNKS, wait_d, 0)

            @pl.when(me == 0)
            def _():
                def body(b, _):
                    u[0, b] = jnp.zeros((half_w, chan_m), BF16)
                    return 0
                lax.fori_loop(0, batch, body, 0)

            for t in range(tiles):
                cols = slice(t * TILE, (t + 1) * TILE)
                recv_moments(ar_down + t, bn_down[:, cols], t * TILE, TILE, count_b)

                def first_h(c, _):
                    rows_at = pl.ds(pl.multiple_of(c * m_rows, m_rows), m_rows)
                    h[rows_at, cols] = norm_relu(zb[rows_at, cols], t * TILE).astype(BF16)
                    return 0
                lax.fori_loop(0, CHUNKS, first_h, 0)

            wait_weight(win, 2)
            wait_weight(wmid, 3)
            wait_weight(wout, 4)

            def block(j, _):
                clear_moments()

                def in_body(c, _):
                    rows_at = pl.ds(pl.multiple_of(c * m_rows, m_rows), m_rows)
                    z = dot(h[rows_at, :], win[j])
                    zb[rows_at, 0:chan_m] = z
                    add_moments(z, 0)
                    return 0
                lax.fori_loop(0, CHUNKS, in_body, 0)
                send_moments(ar_in + j, 0, chan_m)
                recv_moments(ar_in + j, bn_in[j], 0, chan_m, count_b)

                def renorm_u(c, _):
                    rows_at = pl.ds(pl.multiple_of(c * m_rows, m_rows), m_rows)
                    sl = pl.ds(c * per_chunk, per_chunk)
                    u[1, sl] = norm_relu(zb[rows_at, 0:chan_m], 0).astype(BF16).reshape(per_chunk, half_w, chan_m)
                    start_pair(*u_copies(c))
                    return 0
                lax.fori_loop(0, CHUNKS, renorm_u, 0)
                clear_moments()

                def mid_body(c, _):
                    wait_halo(u_copies, c)
                    rows_at = pl.ds(pl.multiple_of(c * m_rows, m_rows), m_rows)
                    sl = pl.ds(c * per_chunk, per_chunk)
                    x = jnp.concatenate([u[r, sl].reshape(m_rows, chan_m) for r in range(3)], axis=1)
                    z = dot(x, wmid[j, :, chan_m:2 * chan_m])
                    z = z + from_left(dot(x, wmid[j, :, 0:chan_m]), half_w)
                    z = z + from_right(dot(x, wmid[j, :, 2 * chan_m:3 * chan_m]), half_w)
                    zb[rows_at, 0:chan_m] = z
                    add_moments(z, 0)
                    return 0
                lax.fori_loop(0, CHUNKS, mid_body, 0)
                send_moments(ar_mid + j, 0, chan_m)
                wait_sends(u_copies)
                recv_moments(ar_mid + j, bn_mid[j], 0, chan_m, count_b)

                clear_moments()
                for t in range(tiles):
                    cols = slice(t * TILE, (t + 1) * TILE)

                    def out_body(c, _):
                        rows_at = pl.ds(pl.multiple_of(c * m_rows, m_rows), m_rows)
                        if t == 0:
                            u2[rows_at, :] = norm_relu(zb[rows_at, 0:chan_m], 0).astype(BF16)
                        z = dot(u2[rows_at, :], wout[j, :, cols])
                        zb[rows_at, cols] = z
                        add_moments(z, t * TILE)
                        return 0
                    lax.fori_loop(0, CHUNKS, out_body, 0)
                    send_moments(ar_out + j * tiles + t, t * TILE, TILE)
                for t in range(tiles):
                    cols = slice(t * TILE, (t + 1) * TILE)
                    recv_moments(ar_out + j * tiles + t, bn_out[j, :, cols], t * TILE, TILE, count_b)

                    def next_h(c, _):
                        rows_at = pl.ds(pl.multiple_of(c * m_rows, m_rows), m_rows)
                        summed = norm(zb[rows_at, cols], t * TILE) + h[rows_at, cols].astype(F32)
                        h[rows_at, cols] = jnp.maximum(summed, 0.0).astype(BF16)
                        return 0
                    lax.fori_loop(0, CHUNKS, next_h, 0)
                return 0
            lax.fori_loop(0, blocks, block, 0)

            done = pltpu.make_async_copy(h, out, sem_out.at[0])
            done.start()
            done.wait()

        scratch = [
            pltpu.VMEM((4, batch, width, chan_a), BF16),
            pltpu.VMEM((3, batch, half_w, chan_m), BF16),
            pltpu.VMEM((points, chan_b), F32),
            pltpu.VMEM((points, chan_b), BF16),
            pltpu.VMEM((points, chan_m), BF16),
            pltpu.VMEM((layers, 3 * chan_a, 3 * chan_a), BF16),
            pltpu.VMEM((9 * chan_a, chan_b), BF16),
            pltpu.VMEM((blocks, chan_b, chan_m), BF16),
            pltpu.VMEM((blocks, 3 * chan_m, 3 * chan_m), BF16),
            pltpu.VMEM((blocks, chan_m, chan_b), BF16),
            pltpu.VMEM((2, 8, chan_b), F32),
            pltpu.VMEM((8, chan_b), F32),
            pltpu.VMEM((2, width, chan_a), F32),
            pltpu.VMEM((ar_total, 1, 2 * TILE), F32),
            pltpu.VMEM((ar_total, groups - 1, 1, 2 * TILE), F32),
            pltpu.SemaphoreType.DMA((5,)),
            pltpu.SemaphoreType.DMA((2, CHUNKS)),
            pltpu.SemaphoreType.DMA((2, CHUNKS)),
            pltpu.SemaphoreType.DMA((2, CHUNKS)),
            pltpu.SemaphoreType.DMA((2, CHUNKS)),
            pltpu.SemaphoreType.DMA((2, CHUNKS)),
            pltpu.SemaphoreType.DMA((ar_total,)),
            pltpu.SemaphoreType.DMA((ar_total,)),
            pltpu.SemaphoreType.DMA((1,)),
        ]
        return kernel, scratch, points

    def forward(images, w_a, bn_a, w_down, bn_down, w_in, bn_in, w_mid, bn_mid, w_out, bn_out):
        batch, rows, width, chan_a = images.shape
        chan_b, chan_m = w_in.shape[1:]
        kernel, scratch, points = make_kernel(batch, rows, width, chan_a, chan_b, chan_m, w_a.shape[0], w_in.shape[0])
        hbm = pl.BlockSpec(memory_space=pl.ANY)
        vmem = pl.BlockSpec(memory_space=pltpu.VMEM)
        res = pl.pallas_call(
            kernel,
            out_shape=jax.ShapeDtypeStruct((points, chan_b), BF16),
            in_specs=[hbm] * 6 + [vmem] * 5,
            out_specs=hbm,
            scratch_shapes=scratch,
            name="conv_stack",
            compiler_params=pltpu.CompilerParams(collective_id=0, has_side_effects=True, vmem_limit_bytes=67043328),
        )(images, w_a, w_down, w_in, w_mid, w_out, bn_a, bn_down, bn_in, bn_mid, bn_out)
        return res.reshape(batch, rows // 2, width // 2, chan_b)

    act_spec = P("dp", "sp", None, None)
    return jax.shard_map(forward, mesh=mesh, in_specs=(act_spec,) + (P(),) * 10, out_specs=act_spec, check_vma=False)
```

time: 726 us -> 281 us (0.39); the launches traced: 715 us -> 280 us
  blocking collectives: 295 us -> 0 us
  Pallas kernels: 0 us -> 272 us
  waiting for transfers between devices: 142 us -> 0 us
  matrix products: 130 us -> 0 us
  other arithmetic: 93.5 us -> 0 us
  starting transfers between devices: 34.3 us -> 0 us
  local copies, waits for them, and re-layouts: 18.7 us -> 8.37 us
    psum x12 -> x0, blocking collectives: 295 us -> none  [batch_norm(): group_moments = lax.psum(part_sums, 'sp') / norm_count]
    pallas_call x0 -> x1, Pallas kernels: none -> 272 us  [forward(): pl.pallas_call(kernel, out_shape=jax.ShapeDtypeStruct((points, chan_b), B...]
    ppermute x11 -> x0, waiting for transfers between devices: 142 us -> none  [the longest x5 74.1 us: conv_same(): from_below = lax.ppermute(hidden[:, :1], 'sp', to_prev)]
    convert_element_type x8 -> x0, other arithmetic: 74 us -> none  [the longest x3 55.7 us: forward(): hidden = jax.nn.relu(summed).astype(jnp.bfloat16)]
    conv_general_dilated x6 -> x0, matrix products: 65.1 us -> none  [the longest x5 51.6 us: conv_same(): lax.conv_general_dilated(padded, weight, (1, 1), ((0, 0), (1, 1)), dimens...]
    dot_general x6 -> x0, matrix products: 64.8 us -> none  [conv_point(): jnp.einsum('bhwc,cd->bhwd', hidden, weight, preferred_element_type=jnp.fl...]
    ppermute x11 -> x0, starting transfers between devices: 34.3 us -> none  [the longest x5 17.2 us: conv_same(): from_above = lax.ppermute(hidden[:, -1:], 'sp', to_next)]
    another operation x16 -> x0, other arithmetic: 16.3 us -> none
  transfers between devices with their start and end apart: 11 -> 0, of which waited for: 11 -> 0; matrix products, arithmetic and copies ran while one was open for 0% -> 0% of each run, Pallas kernels for 0% -> 0%
where the time goes in v1:
time: 281 us; the launch traced here: 280 us
  Pallas kernels  272 us (97%)
  local copies, waits for them, and re-layouts  8.37 us (3%)
    pallas_call x1, Pallas kernels, forward(): pl.pallas_call(kernel, out_shape=jax.ShapeDtypeStruct((points, chan_b), B...  272 us
    unnamed x1, local copies, waits for them, and re-layouts  8.37 us

profile of v1, /device:TPU:21, one launch (start us, length us, event | category | flops | bytes accessed | tf_op | source)
XLA Modules:
  0.0 280.4 jit_solution(8428468810130443404)
XLA Ops:
  0.0 272.0 %conv_stack.1 = bf16[4096,1024]{1,0:T(8,128)(2,1)} custom-call(bf16[32,2,256,128]{3,2,1,0:T(8,128)(2,1)} %images.1, bf16[2,3,3,128,128]{4,3,2,1,0:T(8,128)(2,1)} %w_a.1, bf16[3,3,128,1024]{3,2,1,0:T(8,128)(2,1)} %w_down.1, bf16[3,1024,256]{2,1,0:T(8,128)(2,1)} %w_in.1, bf16[3,3,3,256,256]{4,3,2,1,0:T(8,128)(2,1)} %w_mid.1, bf16[3,256,1024]{2,1,0:T(8,128)(2,1)} %w_out.1, ...), custom_call_target="tpu_custom_call" | custom-call | tf_op jit(solution)/shard_map/conv_stack/pallas_call | solution.py:413
  272.0 8.4 %copy.14 = bf16[32,1,128,1024]{3,2,1,0:T(8,128)(2,1)} copy(bf16[32,1,128,1024]{3,2,1,0:T(8,128)(2,1)} %bitcast.3) | data formatting | bytes 16777216

commit v2 on v1

--- a/solution.py
+++ b/solution.py
@@ -6,7 +6,10 @@
 from jax.sharding import PartitionSpec as P
 
 NORM_EPS = 1e-5
-CHUNKS = 8
+CHUNKS = 16
+ROW_STEPS = 8
+IN_STEPS = 4
+OUT_STEPS = 2
 TILE = 256
 F32 = jnp.float32
 BF16 = jnp.bfloat16
@@ -23,16 +26,16 @@
         half_b = batch // 2
         tiles = chan_b // TILE
         m_rows = points // CHUNKS
+        pair_a = 2 * chan_a
         count_a = float(batch * rows * width * groups)
         count_b = float(points * groups)
-        ar_down = layers
-        ar_in = ar_down + tiles
+        ar_in = layers
         ar_mid = ar_in + blocks
         ar_out = ar_mid + blocks
-        ar_total = ar_out + blocks * tiles
-
-        def kernel(images, w_a, w_down, w_in, w_mid, w_out, bn_a, bn_down, bn_in, bn_mid, bn_out, out,
-                   xa, u, zb, h, u2, wa, wd, win, wmid, wout, st, nrm, tmp, arsend, arbuf,
+        ar_total = ar_out + (blocks + 1) * tiles
+
+        def kernel(images, w_a, w_down, w_in, w_mid, w_out, bn_a, bn_down, bn_in, bn_mid, bn_out, h_out, u2_out, nrm_out,
+                   xa, u, zb, h, u2, wa, wd, win, wmid, wout, st, nrm, prm, tmp, arsend, arbuf,
                    sem_w, sem_img, a_send, a_recv, u_send, u_recv, ar_ssem, ar_rsem, sem_out):
             me = lax.axis_index("sp")
             has_prev = me > 0
@@ -52,11 +55,29 @@
                 for r in range(2):
                     img_copy(c, r).start()
                 return 0
-            for dy in range(3):
+            lax.fori_loop(0, CHUNKS, load_images, 0)
+
+            def wa_copies(start):
+                for l in range(layers):
+                    for dx in range(3):
+                        for r in range(2):
+                            for dy in range(3):
+                                part = wa.at[l, pl.ds((r + dy) * chan_a, chan_a), pl.ds((2 * dx + r) * chan_a, chan_a)]
+                                copy = pltpu.make_async_copy(w_a.at[l, dy, dx], part, sem_w.at[0])
+                                if start:
+                                    copy.start()
+                                else:
+                                    copy.wait()
+            wa_copies(True)
+
+            for l in range(layers):
                 for dx in range(3):
-                    for l in range(layers):
-                        pltpu.make_async_copy(w_a.at[l, dy, dx], wa.at[l, pl.ds(dy * chan_a, chan_a), pl.ds(dx * chan_a, chan_a)], sem_w.at[0]).start()
-            lax.fori_loop(0, CHUNKS, load_images, 0)
+                    for r in range(2):
+                        wa[l, 3 * (1 - r) * chan_a:(3 * (1 - r) + 1) * chan_a, (2 * dx + r) * chan_a:(2 * dx + r + 1) * chan_a] = jnp.zeros((chan_a, chan_a), BF16)
+            nrm[...] = jnp.zeros_like(nrm)
+            prm[0] = bn_down[...]
+            for j in range(blocks):
+                prm[j + 1] = bn_out[j]
 
             barrier = pltpu.get_barrier_semaphore()
             for k in peers:
@@ -127,24 +148,56 @@
             def ar_copy(a, k):
                 return remote(arsend.at[a], arbuf.at[a, k - 1], ar_ssem.at[a], ar_rsem.at[a], lax.rem(me + k, groups))
 
-            def send_moments(a, lo, wide):
-                s = jnp.sum(st[0, :, lo:lo + wide], axis=0, keepdims=True)
-                q = jnp.sum(st[1, :, lo:lo + wide], axis=0, keepdims=True)
-                both = jnp.concatenate([s, q] * (TILE // wide), axis=1)
-                arsend[a] = both
+            def pack_moments(a, lo):
+                s = jnp.sum(st[0, :, lo:lo + TILE], axis=0, keepdims=True)
+                q = jnp.sum(st[1, :, lo:lo + TILE], axis=0, keepdims=True)
+                arsend[a] = jnp.concatenate([s, q], axis=1)
+
+            def send_moments(a, lo):
+                pack_moments(a, lo)
                 for k in peers:
                     ar_copy(a, k).start()
 
-            def recv_moments(a, params, lo, wide, count):
-                pltpu.make_async_copy(arbuf.at[a], arbuf.at[a], ar_rsem.at[a]).wait()
+            def ar_wait(a, sem):
+                pltpu.make_async_copy(arbuf.at[a], arbuf.at[a], sem.at[a]).wait()
+
+            def use_moments(a, params, lo, count):
                 total = jnp.sum(arbuf[a], axis=0) + arsend[a]
-                m = total[:, :wide] / count
-                q = total[:, wide:2 * wide] / count
-                v = q - m * m
-                nrm[0:1, lo:lo + wide] = m
-                nrm[1:2, lo:lo + wide] = params[0:1] * lax.rsqrt(v + NORM_EPS)
-                nrm[2:3, lo:lo + wide] = params[1:2]
-                pltpu.make_async_copy(arbuf.at[a], arbuf.at[a], ar_ssem.at[a]).wait()
+                s = total[:, :TILE]
+                q = total[:, TILE:]
+                if count == count_a:
+                    s = s[:, :chan_a] + s[:, chan_a:]
+                    q = q[:, :chan_a] + q[:, chan_a:]
+                m = s / count
+                v = q / count - m * m
+                scale = params[0:1] * lax.rsqrt(v + NORM_EPS)
+                for at in range(lo, lo + TILE, m.shape[1]):
+                    nrm[0:1, at:at + m.shape[1]] = m
+                    nrm[1:2, at:at + m.shape[1]] = scale
+                    nrm[2:3, at:at + m.shape[1]] = params[1:2]
+
+            def recv_moments(a, params, lo, count):
+                ar_wait(a, ar_rsem)
+                use_moments(a, params, lo, count)
+                ar_wait(a, ar_ssem)
+
+            def tile_waits(j, t, sem):
+                first = ar_out + j * tiles
+
+                if t == 0:
+                    @pl.when(j == 0)
+                    def _():
+                        every = arbuf.at[pl.ds(ar_out, tiles)]
+                        pltpu.make_async_copy(every, every, sem.at[ar_out]).wait()
+
+                @pl.when(j > 0)
+                def _():
+                    ar_wait(first + t, sem)
+
+            def recv_tile(j, t):
+                tile_waits(j, t, ar_rsem)
+                use_moments(ar_out + j * tiles + t, prm[j, :, t * TILE:(t + 1) * TILE], t * TILE, count_b)
+                tile_waits(j, t, ar_ssem)
 
             def norm(z, lo):
                 wide = z.shape[-1]
@@ -196,7 +249,12 @@
             def wait_weight(ref, i):
                 pltpu.make_async_copy(ref, ref, sem_w.at[i]).wait()
 
-            wait_weight(wa, 0)
+            wa_copies(False)
+
+            def zero_h(c, _):
+                h[pl.ds(pl.multiple_of(c * m_rows, m_rows), m_rows), :] = jnp.zeros((m_rows, chan_b), BF16)
+                return 0
+            lax.fori_loop(0, CHUNKS, zero_h, 0)
 
             def conv_a(l):
                 clear_moments()
@@ -211,29 +269,30 @@
                                 for r in range(2):
                                     img_copy(c, r).wait()
                             wait_halo(lambda c: a_copies(c, l == 0), c)
-                        for r in range(2):
-                            x = jnp.concatenate([xa[r, b], xa[r + 1, b], xa[r + 2, b]], axis=1)
-                            z = dot(x, wa[l, :, chan_a:2 * chan_a])
-                            z = z + from_left(dot(x, wa[l, :, 0:chan_a]), width)
-                            z = z + from_right(dot(x, wa[l, :, 2 * chan_a:3 * chan_a]), width)
-                            lane = (2 * r + hb) * chan_a
-                            zb[pl.ds(pl.multiple_of(i * width, width), width), lane:lane + chan_a] = z
-                            add_moments(z, 0)
+                        x = jnp.concatenate([xa[r, b] for r in range(4)], axis=1)
+                        z = dot(x, wa[l, :, pair_a:2 * pair_a])
+                        z = z + from_left(dot(x, wa[l, :, 0:pair_a]), width)
+                        z = z + from_right(dot(x, wa[l, :, 2 * pair_a:3 * pair_a]), width)
+                        zb[pl.ds(pl.multiple_of(i * width, width), width), hb * pair_a:(hb + 1) * pair_a] = z
+                        add_moments(z, 0)
                         return 0
                     lax.fori_loop(0, half_b, body, 0)
-                send_moments(l, 0, chan_a)
+                send_moments(l, 0)
                 wait_sends(lambda c: a_copies(c, l == 0))
-                recv_moments(l, bn_a[l], 0, chan_a, count_a)
+                recv_moments(l, bn_a[l], 0, count_a)
+
+            def normed_pair(hb, i):
+                z = zb[pl.ds(pl.multiple_of(i * width, width), width), hb * pair_a:(hb + 1) * pair_a]
+                return norm_relu(z, 0)
 
             conv_a(0)
             for l in range(1, layers):
                 for hb in range(2):
                     def renorm(i, _):
                         b = hb * half_b + i
-                        for r in range(2):
-                            lane = (2 * r + hb) * chan_a
-                            z = zb[pl.ds(pl.multiple_of(i * width, width), width), lane:lane + chan_a]
-                            xa[1 + r, b] = norm_relu(z, 0).astype(BF16)
+                        y = normed_pair(hb, i).astype(BF16)
+                        xa[1, b] = y[:, :chan_a]
+                        xa[2, b] = y[:, chan_a:]
 
                         @pl.when(lax.rem(b, per_chunk) == per_chunk - 1)
                         def _():
@@ -245,10 +304,9 @@
             for hb in range(2):
                 def pair_up(i, _):
                     b = hb * half_b + i
+                    y = normed_pair(hb, i)
                     for r in range(2):
-                        lane = (2 * r + hb) * chan_a
-                        z = zb[pl.ds(pl.multiple_of(i * width, width), width), lane:lane + chan_a]
-                        tmp[r] = norm_relu(z, 0)
+                        tmp[r] = y[:, r * chan_a:(r + 1) * chan_a]
                         u[r, b, :, 0:chan_a] = tmp[r, pl.ds(0, half_w, stride=2), :].astype(BF16)
                         u[r, b, :, chan_a:2 * chan_a] = tmp[r, pl.ds(1, half_w, stride=2), :].astype(BF16)
 
@@ -277,7 +335,10 @@
                 return 0
             lax.fori_loop(0, CHUNKS, down_body, 0)
             for t in range(tiles):
-                send_moments(ar_down + t, t * TILE, TILE)
+                pack_moments(ar_out + t, t * TILE)
+            every_tile = pl.ds(ar_out, tiles)
+            for k in peers:
+                remote(arsend.at[every_tile], arbuf.at[every_tile, k - 1], ar_ssem.at[ar_out], ar_rsem.at[ar_out], lax.rem(me + k, groups)).start()
 
             def wait_d(c, _):
                 @pl.when(has_prev)
@@ -293,32 +354,48 @@
                     return 0
                 lax.fori_loop(0, batch, body, 0)
 
-            for t in range(tiles):
-                cols = slice(t * TILE, (t + 1) * TILE)
-                recv_moments(ar_down + t, bn_down[:, cols], t * TILE, TILE, count_b)
-
-                def first_h(c, _):
-                    rows_at = pl.ds(pl.multiple_of(c * m_rows, m_rows), m_rows)
-                    h[rows_at, cols] = norm_relu(zb[rows_at, cols], t * TILE).astype(BF16)
-                    return 0
-                lax.fori_loop(0, CHUNKS, first_h, 0)
-
             wait_weight(win, 2)
             wait_weight(wmid, 3)
             wait_weight(wout, 4)
 
+            def next_h(rows_at, t):
+                cols = slice(t * TILE, (t + 1) * TILE)
+                summed = norm(zb[rows_at, cols], t * TILE) + h[rows_at, cols].astype(F32)
+                return jnp.maximum(summed, 0.0).astype(BF16)
+
+            def h_copy():
+                return pltpu.make_async_copy(h, h_out, sem_out.at[0])
+
+            def u2_copy():
+                return pltpu.make_async_copy(u2, u2_out, sem_out.at[1])
+
             def block(j, _):
+                for t in range(tiles - 1):
+                    recv_tile(j, t)
+
+                    def tile_body(c, _):
+                        rows_at = pl.ds(pl.multiple_of(c * (points // ROW_STEPS), points // ROW_STEPS), points // ROW_STEPS)
+                        h[rows_at, t * TILE:(t + 1) * TILE] = next_h(rows_at, t)
+                        return 0
+                    lax.fori_loop(0, ROW_STEPS, tile_body, 0)
+                recv_tile(j, tiles - 1)
                 clear_moments()
 
                 def in_body(c, _):
-                    rows_at = pl.ds(pl.multiple_of(c * m_rows, m_rows), m_rows)
-                    z = dot(h[rows_at, :], win[j])
+                    rows_at = pl.ds(pl.multiple_of(c * (points // IN_STEPS), points // IN_STEPS), points // IN_STEPS)
+                    last = next_h(rows_at, tiles - 1)
+                    h[rows_at, chan_b - TILE:chan_b] = last
+                    z = dot(jnp.concatenate([h[rows_at, 0:chan_b - TILE], last], axis=1), win[j])
                     zb[rows_at, 0:chan_m] = z
                     add_moments(z, 0)
                     return 0
-                lax.fori_loop(0, CHUNKS, in_body, 0)
-                send_moments(ar_in + j, 0, chan_m)
-                recv_moments(ar_in + j, bn_in[j], 0, chan_m, count_b)
+                lax.fori_loop(0, IN_STEPS, in_body, 0)
+                send_moments(ar_in + j, 0)
+
+                @pl.when(j == blocks - 1)
+                def _():
+                    h_copy().start()
+                recv_moments(ar_in + j, bn_in[j], 0, count_b)
 
                 def renorm_u(c, _):
                     rows_at = pl.ds(pl.multiple_of(c * m_rows, m_rows), m_rows)
@@ -341,40 +418,38 @@
                     add_moments(z, 0)
                     return 0
                 lax.fori_loop(0, CHUNKS, mid_body, 0)
-                send_moments(ar_mid + j, 0, chan_m)
+                send_moments(ar_mid + j, 0)
                 wait_sends(u_copies)
-                recv_moments(ar_mid + j, bn_mid[j], 0, chan_m, count_b)
+                recv_moments(ar_mid + j, bn_mid[j], 0, count_b)
 
                 clear_moments()
                 for t in range(tiles):
                     cols = slice(t * TILE, (t + 1) * TILE)
 
                     def out_body(c, _):
-                        rows_at = pl.ds(pl.multiple_of(c * m_rows, m_rows), m_rows)
+                        rows_at = pl.ds(pl.multiple_of(c * (points // OUT_STEPS), points // OUT_STEPS), points // OUT_STEPS)
                         if t == 0:
                             u2[rows_at, :] = norm_relu(zb[rows_at, 0:chan_m], 0).astype(BF16)
                         z = dot(u2[rows_at, :], wout[j, :, cols])
                         zb[rows_at, cols] = z
                         add_moments(z, t * TILE)
                         return 0
-                    lax.fori_loop(0, CHUNKS, out_body, 0)
-                    send_moments(ar_out + j * tiles + t, t * TILE, TILE)
-                for t in range(tiles):
-                    cols = slice(t * TILE, (t + 1) * TILE)
-                    recv_moments(ar_out + j * tiles + t, bn_out[j, :, cols], t * TILE, TILE, count_b)
-
-                    def next_h(c, _):
-                        rows_at = pl.ds(pl.multiple_of(c * m_rows, m_rows), m_rows)
-                        summed = norm(zb[rows_at, cols], t * TILE) + h[rows_at, cols].astype(F32)
-                        h[rows_at, cols] = jnp.maximum(summed, 0.0).astype(BF16)
-                        return 0
-                    lax.fori_loop(0, CHUNKS, next_h, 0)
+                    lax.fori_loop(0, OUT_STEPS, out_body, 0)
+                    send_moments(ar_out + (j + 1) * tiles + t, t * TILE)
+                    if t == 0:
+                        @pl.when(j == blocks - 1)
+                        def _():
+                            u2_copy().start()
                 return 0
             lax.fori_loop(0, blocks, block, 0)
 
-            done = pltpu.make_async_copy(h, out, sem_out.at[0])
-            done.start()
-            done.wait()
+            for t in range(tiles):
+                recv_tile(blocks, t)
+            nrm_copy = pltpu.make_async_copy(nrm, nrm_out, sem_out.at[2])
+            nrm_copy.start()
+            h_copy().wait()
+            u2_copy().wait()
+            nrm_copy.wait()
 
         scratch = [
             pltpu.VMEM((4, batch, width, chan_a), BF16),
@@ -382,13 +457,14 @@
             pltpu.VMEM((points, chan_b), F32),
             pltpu.VMEM((points, chan_b), BF16),
             pltpu.VMEM((points, chan_m), BF16),
-            pltpu.VMEM((layers, 3 * chan_a, 3 * chan_a), BF16),
+            pltpu.VMEM((layers, 4 * chan_a, 6 * chan_a), BF16),
             pltpu.VMEM((9 * chan_a, chan_b), BF16),
             pltpu.VMEM((blocks, chan_b, chan_m), BF16),
             pltpu.VMEM((blocks, 3 * chan_m, 3 * chan_m), BF16),
             pltpu.VMEM((blocks, chan_m, chan_b), BF16),
             pltpu.VMEM((2, 8, chan_b), F32),
             pltpu.VMEM((8, chan_b), F32),
+            pltpu.VMEM((blocks + 1, 2, chan_b), F32),
             pltpu.VMEM((2, width, chan_a), F32),
             pltpu.VMEM((ar_total, 1, 2 * TILE), F32),
             pltpu.VMEM((ar_total, groups - 1, 1, 2 * TILE), F32),
@@ -400,7 +476,7 @@
             pltpu.SemaphoreType.DMA((2, CHUNKS)),
             pltpu.SemaphoreType.DMA((ar_total,)),
             pltpu.SemaphoreType.DMA((ar_total,)),
-            pltpu.SemaphoreType.DMA((1,)),
+            pltpu.SemaphoreType.DMA((3,)),
         ]
         return kernel, scratch, points
 
@@ -410,15 +486,39 @@
         kernel, scratch, points = make_kernel(batch, rows, width, chan_a, chan_b, chan_m, w_a.shape[0], w_in.shape[0])
         hbm = pl.BlockSpec(memory_space=pl.ANY)
         vmem = pl.BlockSpec(memory_space=pltpu.VMEM)
-        res = pl.pallas_call(
+        h_last, branch, moments = pl.pallas_call(
             kernel,
-            out_shape=jax.ShapeDtypeStruct((points, chan_b), BF16),
+            out_shape=(jax.ShapeDtypeStruct((points, chan_b), BF16),
+                       jax.ShapeDtypeStruct((points, chan_m), BF16),
+                       jax.ShapeDtypeStruct((8, chan_b), F32)),
             in_specs=[hbm] * 6 + [vmem] * 5,
-            out_specs=hbm,
+            out_specs=(hbm, hbm, hbm),
             scratch_shapes=scratch,
             name="conv_stack",
             compiler_params=pltpu.CompilerParams(collective_id=0, has_side_effects=True, vmem_limit_bytes=67043328),
         )(images, w_a, w_down, w_in, w_mid, w_out, bn_a, bn_down, bn_in, bn_mid, bn_out)
+
+        step = points // ROW_STEPS
+        last = w_out.shape[0] - 1
+
+        def finish(branch_ref, h_ref, w_ref, nrm_ref, out_ref):
+            for t in range(chan_b // TILE):
+                cols = slice(t * TILE, (t + 1) * TILE)
+                z = jnp.dot(branch_ref[...], w_ref[0, :, cols], preferred_element_type=F32)
+                normed = (z - nrm_ref[0:1, cols]) * nrm_ref[1:2, cols] + nrm_ref[2:3, cols]
+                out_ref[:, cols] = jnp.maximum(normed + h_ref[:, cols].astype(F32), 0.0).astype(BF16)
+
+        res = pl.pallas_call(
+            finish,
+            grid=(ROW_STEPS,),
+            out_shape=jax.ShapeDtypeStruct((points, chan_b), BF16),
+            in_specs=[pl.BlockSpec((step, chan_m), lambda i: (i, 0)),
+                      pl.BlockSpec((step, chan_b), lambda i: (i, 0)),
+                      pl.BlockSpec((1, chan_m, chan_b), lambda i: (last, 0, 0)),
+                      pl.BlockSpec((8, chan_b), lambda i: (0, 0))],
+            out_specs=pl.BlockSpec((step, chan_b), lambda i: (i, 0)),
+            name="last_norm",
+        )(branch, h_last, w_out, moments)
         return res.reshape(batch, rows // 2, width // 2, chan_b)
 
     act_spec = P("dp", "sp", None, None)

time: 281 us -> 262 us (0.932)
  Pallas kernels: 272 us -> 262 us
  local copies, waits for them, and re-layouts: 8.37 us -> 0 us
    pallas_call x1 -> x2, Pallas kernels: 272 us -> 262 us  [the longest x1 251 us: forward(): pl.pallas_call(kernel, out_shape=(jax.ShapeDtypeStruct((points, chan_b),...]
    unnamed x1 -> x0, local copies, waits for them, and re-layouts: 8.37 us -> none
where the time goes in v2:
time: 262 us
  Pallas kernels  262 us (100%)
    pallas_call x1, Pallas kernels, forward(): pl.pallas_call(kernel, out_shape=(jax.ShapeDtypeStruct((points, chan_b),...  251 us
    pallas_call x1, Pallas kernels, forward(): pl.pallas_call(finish, grid=(ROW_STEPS,), out_shape=jax.ShapeDtypeStruct(...  11.6 us

profile of v2, /device:TPU:21, one launch (start us, length us, event | category | flops | bytes accessed | tf_op | source)
XLA Modules:
  0.0 262.1 jit_solution(15551745893640895362)
XLA Ops:
  0.0 250.5 %conv_stack.1 = (bf16[4096,1024]{1,0:T(8,128)(2,1)}, bf16[4096,256]{1,0:T(8,128)(2,1)}, f32[8,1024]{1,0:T(8,128)}) custom-call(bf16[32,2,256,128]{3,2,1,0:T(8,128)(2,1)} %images.1, bf16[2,3,3,128,128]{4,3,2,1,0:T(8,128)(2,1)} %w_a.1, bf16[3,3,128,1024]{3,2,1,0:T(8,128)(2,1)} %w_down.1, bf16[3,1024,256]{2,1,0:T(8,128)(2,1)} %w_in.1, ...), custom_call_target="tpu_custom_call" | custom-call | tf_op jit(solution)/shard_map/conv_stack/pallas_call | solution.py:489
  250.5 11.6 %last_norm.1 = bf16[4096,1024]{1,0:T(8,128)(2,1)} custom-call(bf16[4096,256]{1,0:T(8,128)(2,1)} %get-tuple-element.8.branch_ref, bf16[4096,1024]{1,0:T(8,128)(2,1)} %get-tuple-element.9.h_ref, bf16[3,256,1024]{2,1,0:T(8,128)(2,1)} %w_ref.1, f32[8,1024]{1,0:T(8,128)} %get-tuple-element.10.nrm_ref), custom_call_target="tpu_custom_call" | custom-call | tf_op jit(solution)/shard_map/last_norm/pallas_call | solution.py:511

commit v3 on v2

--- a/solution.py
+++ b/solution.py
@@ -10,6 +10,9 @@
 ROW_STEPS = 8
 IN_STEPS = 4
 OUT_STEPS = 2
+LAST_STEPS = 4
+EARLY_A = 4
+EARLY_B = 4
 TILE = 256
 F32 = jnp.float32
 BF16 = jnp.bfloat16
@@ -27,6 +30,8 @@
         tiles = chan_b // TILE
         m_rows = points // CHUNKS
         pair_a = 2 * chan_a
+        early_a = EARLY_A // per_chunk
+        early_b = EARLY_B // per_chunk
         count_a = float(batch * rows * width * groups)
         count_b = float(points * groups)
         ar_in = layers
@@ -35,8 +40,8 @@
         ar_total = ar_out + (blocks + 1) * tiles
 
         def kernel(images, w_a, w_down, w_in, w_mid, w_out, bn_a, bn_down, bn_in, bn_mid, bn_out, h_out, u2_out, nrm_out,
-                   xa, u, zb, h, u2, wa, wd, win, wmid, wout, st, nrm, prm, tmp, arsend, arbuf,
-                   sem_w, sem_img, a_send, a_recv, u_send, u_recv, ar_ssem, ar_rsem, sem_out):
+                   xa, u, zb, h, u2, wa, wd, win, wmid, wout, st, nrm, prm, tmp, arsend, arbuf, ez_a, ez_d, ez_b,
+                   sem_w, sem_img, a_send, a_recv, u_send, u_recv, ar_ssem, ar_rsem, e_send, e_recv, sem_out):
             me = lax.axis_index("sp")
             has_prev = me > 0
             has_next = me < groups - 1
@@ -111,7 +116,7 @@
                 def _():
                     down.start()
 
-            def wait_sends(pair_of):
+            def wait_sends(pair_of, first=0):
                 def body(c, _):
                     up, down = pair_of(c)
 
@@ -123,7 +128,51 @@
                     def _():
                         down.wait_send()
                     return 0
-                lax.fori_loop(0, CHUNKS, body, 0)
+                lax.fori_loop(first, CHUNKS, body, 0)
+
+            def early_a_copies(l):
+                rows_at = pl.ds(0, EARLY_A * width)
+                if l == layers - 1:
+                    return remote(zb.at[rows_at, pl.ds(0, chan_a)], ez_d, e_send.at[l, 0], e_recv.at[l, 1], prev), None
+                up = remote(zb.at[rows_at, pl.ds(0, chan_a)], ez_a.at[l, 1], e_send.at[l, 0], e_recv.at[l, 1], prev)
+                down = remote(zb.at[rows_at, pl.ds(chan_a, chan_a)], ez_a.at[l, 0], e_send.at[l, 1], e_recv.at[l, 0], nxt)
+                return up, down
+
+            def early_b_copies():
+                src = zb.at[pl.ds(0, EARLY_B * half_w), pl.ds(0, chan_m)]
+                up = remote(src, ez_b.at[1], e_send.at[layers, 0], e_recv.at[layers, 1], prev)
+                down = remote(src, ez_b.at[0], e_send.at[layers, 1], e_recv.at[layers, 0], nxt)
+                return up, down
+
+            def start_early(up, down):
+                @pl.when(has_prev)
+                def _():
+                    up.start()
+                if down is not None:
+                    @pl.when(has_next)
+                    def _():
+                        down.start()
+
+            def sent_early(up, down):
+                @pl.when(has_prev)
+                def _():
+                    up.wait_send()
+                if down is not None:
+                    @pl.when(has_next)
+                    def _():
+                        down.wait_send()
+
+            def take_early(up, down, from_prev, from_next, count):
+                if down is not None:
+                    @pl.when(has_prev)
+                    def _():
+                        down.wait_recv()
+                        lax.fori_loop(0, count, from_prev, 0)
+
+                @pl.when(has_next)
+                def _():
+                    up.wait_recv()
+                    lax.fori_loop(0, count, from_next, 0)
 
             def wait_halo(pair_of, c):
                 up, down = pair_of(c)
@@ -141,9 +190,11 @@
 
             def add_moments(z, lo):
                 wide = z.shape[-1]
-                z8 = z.reshape(z.shape[0] // 8, 8, wide)
-                st[0, :, lo:lo + wide] += jnp.sum(z8, axis=0)
-                st[1, :, lo:lo + wide] += jnp.sum(z8 * z8, axis=0)
+                part = min(512, z.shape[0])
+                for p in range(0, z.shape[0], part):
+                    z8 = z[p:p + part].reshape(part // 8, 8, wide)
+                    st[0, :, lo:lo + wide] += jnp.sum(z8, axis=0)
+                    st[1, :, lo:lo + wide] += jnp.sum(z8 * z8, axis=0)
 
             def ar_copy(a, k):
                 return remote(arsend.at[a], arbuf.at[a, k - 1], ar_ssem.at[a], ar_rsem.at[a], lax.rem(me + k, groups))
@@ -263,7 +314,7 @@
                         b = hb * half_b + i
                         c = b // per_chunk
 
-                        @pl.when(lax.rem(b, per_chunk) == 0)
+                        @pl.when(jnp.logical_and(lax.rem(b, per_chunk) == 0, c >= (early_a if l else 0)))
                         def _():
                             if l == 0:
                                 for r in range(2):
@@ -278,7 +329,8 @@
                         return 0
                     lax.fori_loop(0, half_b, body, 0)
                 send_moments(l, 0)
-                wait_sends(lambda c: a_copies(c, l == 0))
+                start_early(*early_a_copies(l))
+                wait_sends(lambda c: a_copies(c, l == 0), early_a if l else 0)
                 recv_moments(l, bn_a[l], 0, count_a)
 
             def normed_pair(hb, i):
@@ -294,11 +346,21 @@
                         xa[1, b] = y[:, :chan_a]
                         xa[2, b] = y[:, chan_a:]
 
-                        @pl.when(lax.rem(b, per_chunk) == per_chunk - 1)
+                        @pl.when(jnp.logical_and(lax.rem(b, per_chunk) == per_chunk - 1, b >= EARLY_A))
                         def _():
                             start_pair(*a_copies(b // per_chunk, False))
                         return 0
                     lax.fori_loop(0, half_b, renorm, 0)
+
+                def early_rows(side, slot):
+                    def body(b, _):
+                        z = ez_a[l - 1, side, pl.ds(pl.multiple_of(b * width, width), width), :]
+                        xa[slot, b] = norm_relu(z, 0).astype(BF16)
+                        return 0
+                    return body
+                up, down = early_a_copies(l - 1)
+                take_early(up, down, early_rows(0, 0), early_rows(1, 3), EARLY_A)
+                sent_early(up, down)
                 conv_a(l)
 
             for hb in range(2):
@@ -310,17 +372,25 @@
                         u[r, b, :, 0:chan_a] = tmp[r, pl.ds(0, half_w, stride=2), :].astype(BF16)
                         u[r, b, :, chan_a:2 * chan_a] = tmp[r, pl.ds(1, half_w, stride=2), :].astype(BF16)
 
-                    @pl.when(jnp.logical_and(lax.rem(b, per_chunk) == per_chunk - 1, has_prev))
+                    @pl.when(jnp.logical_and(jnp.logical_and(lax.rem(b, per_chunk) == per_chunk - 1, b >= EARLY_A), has_prev))
                     def _():
                         d_copy(b // per_chunk).start()
                     return 0
                 lax.fori_loop(0, half_b, pair_up, 0)
 
+            def early_pair(b, _):
+                tmp[0] = norm_relu(ez_d[pl.ds(pl.multiple_of(b * width, width), width), :], 0)
+                u[2, b, :, 0:chan_a] = tmp[0, pl.ds(0, half_w, stride=2), :].astype(BF16)
+                u[2, b, :, chan_a:2 * chan_a] = tmp[0, pl.ds(1, half_w, stride=2), :].astype(BF16)
+                return 0
+            up, down = early_a_copies(layers - 1)
+            take_early(up, down, None, early_pair, EARLY_A)
+            sent_early(up, down)
             wait_weight(wd, 1)
             clear_moments()
 
             def down_body(c, _):
-                @pl.when(has_next)
+                @pl.when(jnp.logical_and(has_next, c >= early_a))
                 def _():
                     d_copy(c).wait_recv()
                 sl = pl.ds(c * per_chunk, per_chunk)
@@ -345,7 +415,7 @@
                 def _():
                     d_copy(c).wait_send()
                 return 0
-            lax.fori_loop(0, CHUNKS, wait_d, 0)
+            lax.fori_loop(early_a, CHUNKS, wait_d, 0)
 
             @pl.when(me == 0)
             def _():
@@ -391,6 +461,7 @@
                     return 0
                 lax.fori_loop(0, IN_STEPS, in_body, 0)
                 send_moments(ar_in + j, 0)
+                start_early(*early_b_copies())
 
                 @pl.when(j == blocks - 1)
                 def _():
@@ -401,13 +472,28 @@
                     rows_at = pl.ds(pl.multiple_of(c * m_rows, m_rows), m_rows)
                     sl = pl.ds(c * per_chunk, per_chunk)
                     u[1, sl] = norm_relu(zb[rows_at, 0:chan_m], 0).astype(BF16).reshape(per_chunk, half_w, chan_m)
-                    start_pair(*u_copies(c))
+
+                    @pl.when(c >= early_b)
+                    def _():
+                        start_pair(*u_copies(c))
                     return 0
                 lax.fori_loop(0, CHUNKS, renorm_u, 0)
+
+                def early_u(side, slot):
+                    def body(b, _):
+                        z = ez_b[side, pl.ds(pl.multiple_of(b * half_w, half_w), half_w), :]
+                        u[slot, b] = norm_relu(z, 0).astype(BF16)
+                        return 0
+                    return body
+                up, down = early_b_copies()
+                take_early(up, down, early_u(0, 0), early_u(1, 2), EARLY_B)
+                sent_early(up, down)
                 clear_moments()
 
                 def mid_body(c, _):
-                    wait_halo(u_copies, c)
+                    @pl.when(c >= early_b)
+                    def _():
+                        wait_halo(u_copies, c)
                     rows_at = pl.ds(pl.multiple_of(c * m_rows, m_rows), m_rows)
                     sl = pl.ds(c * per_chunk, per_chunk)
                     x = jnp.concatenate([u[r, sl].reshape(m_rows, chan_m) for r in range(3)], axis=1)
@@ -419,7 +505,7 @@
                     return 0
                 lax.fori_loop(0, CHUNKS, mid_body, 0)
                 send_moments(ar_mid + j, 0)
-                wait_sends(u_copies)
+                wait_sends(u_copies, early_b)
                 recv_moments(ar_mid + j, bn_mid[j], 0, count_b)
 
                 clear_moments()
@@ -468,6 +554,9 @@
             pltpu.VMEM((2, width, chan_a), F32),
             pltpu.VMEM((ar_total, 1, 2 * TILE), F32),
             pltpu.VMEM((ar_total, groups - 1, 1, 2 * TILE), F32),
+            pltpu.VMEM((layers - 1, 2, EARLY_A * width, chan_a), F32),
+            pltpu.VMEM((EARLY_A * width, chan_a), F32),
+            pltpu.VMEM((2, EARLY_B * half_w, chan_m), F32),
             pltpu.SemaphoreType.DMA((5,)),
             pltpu.SemaphoreType.DMA((2, CHUNKS)),
             pltpu.SemaphoreType.DMA((2, CHUNKS)),
@@ -476,6 +565,8 @@
             pltpu.SemaphoreType.DMA((2, CHUNKS)),
             pltpu.SemaphoreType.DMA((ar_total,)),
             pltpu.SemaphoreType.DMA((ar_total,)),
+            pltpu.SemaphoreType.DMA((layers + 1, 2)),
+            pltpu.SemaphoreType.DMA((layers + 1, 2)),
             pltpu.SemaphoreType.DMA((3,)),
         ]
         return kernel, scratch, points
@@ -498,7 +589,7 @@
             compiler_params=pltpu.CompilerParams(collective_id=0, has_side_effects=True, vmem_limit_bytes=67043328),
         )(images, w_a, w_down, w_in, w_mid, w_out, bn_a, bn_down, bn_in, bn_mid, bn_out)
 
-        step = points // ROW_STEPS
+        step = points // LAST_STEPS
         last = w_out.shape[0] - 1
 
         def finish(branch_ref, h_ref, w_ref, nrm_ref, out_ref):
@@ -510,7 +601,7 @@
 
         res = pl.pallas_call(
             finish,
-            grid=(ROW_STEPS,),
+            grid=(LAST_STEPS,),
             out_shape=jax.ShapeDtypeStruct((points, chan_b), BF16),
             in_specs=[pl.BlockSpec((step, chan_m), lambda i: (i, 0)),
                       pl.BlockSpec((step, chan_b), lambda i: (i, 0)),

time: 262 us -> 252 us (0.962)
  Pallas kernels: 262 us -> 251 us
    pallas_call x1, Pallas kernels: 251 us -> 242 us  [forward(): pl.pallas_call(kernel, out_shape=(jax.ShapeDtypeStruct((points, chan_b),...]
where the time goes in v3:
time: 252 us; the launch traced here: 251 us
  Pallas kernels  251 us (100%)
    pallas_call x1, Pallas kernels, forward(): pl.pallas_call(kernel, out_shape=(jax.ShapeDtypeStruct((points, chan_b),...  242 us
    pallas_call x1, Pallas kernels, forward(): pl.pallas_call(finish, grid=(LAST_STEPS,), out_shape=jax.ShapeDtypeStruct...  9.69 us

profile of v3, /device:TPU:21, one launch (start us, length us, event | category | flops | bytes accessed | tf_op | source)
XLA Modules:
  0.0 251.4 jit_solution(8207037204522515759)
XLA Ops:
  0.0 241.7 %conv_stack.1 = (bf16[4096,1024]{1,0:T(8,128)(2,1)}, bf16[4096,256]{1,0:T(8,128)(2,1)}, f32[8,1024]{1,0:T(8,128)}) custom-call(bf16[32,2,256,128]{3,2,1,0:T(8,128)(2,1)} %images.1, bf16[2,3,3,128,128]{4,3,2,1,0:T(8,128)(2,1)} %w_a.1, bf16[3,3,128,1024]{3,2,1,0:T(8,128)(2,1)} %w_down.1, bf16[3,1024,256]{2,1,0:T(8,128)(2,1)} %w_in.1, ...), custom_call_target="tpu_custom_call" | custom-call | tf_op jit(solution)/shard_map/conv_stack/pallas_call | solution.py:580
  241.7 9.7 %last_norm.1 = bf16[4096,1024]{1,0:T(8,128)(2,1)} custom-call(bf16[4096,256]{1,0:T(8,128)(2,1)} %get-tuple-element.8.branch_ref, bf16[4096,1024]{1,0:T(8,128)(2,1)} %get-tuple-element.9.h_ref, bf16[3,256,1024]{2,1,0:T(8,128)(2,1)} %w_ref.1, f32[8,1024]{1,0:T(8,128)} %get-tuple-element.10.nrm_ref), custom_call_target="tpu_custom_call" | custom-call | tf_op jit(solution)/shard_map/last_norm/pallas_call | solution.py:602

commit v4 on v3

--- a/solution.py
+++ b/solution.py
@@ -34,6 +34,7 @@
         early_b = EARLY_B // per_chunk
         count_a = float(batch * rows * width * groups)
         count_b = float(points * groups)
+        messages = tuple((t,) for t in range(tiles))
         ar_in = layers
         ar_mid = ar_in + blocks
         ar_out = ar_mid + blocks
@@ -51,6 +52,10 @@
             def remote(src, dst, ssem, rsem, dev):
                 return pltpu.make_async_remote_copy(src_ref=src, dst_ref=dst, send_sem=ssem, recv_sem=rsem,
                                                     device_id={"sp": dev}, device_id_type=pl.DeviceIdType.MESH)
+
+            barrier = pltpu.get_barrier_semaphore()
+            for k in peers:
+                pl.semaphore_signal(barrier, inc=1, device_id={"sp": lax.rem(me + k, groups)}, device_id_type=pl.DeviceIdType.MESH)
 
             def img_copy(c, r):
                 sl = pl.ds(c * per_chunk, per_chunk)
@@ -84,9 +89,6 @@
             for j in range(blocks):
                 prm[j + 1] = bn_out[j]
 
-            barrier = pltpu.get_barrier_semaphore()
-            for k in peers:
-                pl.semaphore_signal(barrier, inc=1, device_id={"sp": lax.rem(me + k, groups)}, device_id_type=pl.DeviceIdType.MESH)
             pl.semaphore_wait(barrier, groups - 1)
 
             def a_copies(c, first):
@@ -232,6 +234,13 @@
                 use_moments(a, params, lo, count)
                 ar_wait(a, ar_ssem)
 
+            def send_tiles(first, ts):
+                for t in ts:
+                    pack_moments(first + t, t * TILE)
+                at = pl.ds(first + ts[0], len(ts))
+                for k in peers:
+                    remote(arsend.at[at], arbuf.at[at, k - 1], ar_ssem.at[first + ts[0]], ar_rsem.at[first + ts[0]], lax.rem(me + k, groups)).start()
+
             def tile_waits(j, t, sem):
                 first = ar_out + j * tiles
 
@@ -241,9 +250,12 @@
                         every = arbuf.at[pl.ds(ar_out, tiles)]
                         pltpu.make_async_copy(every, every, sem.at[ar_out]).wait()
 
-                @pl.when(j > 0)
-                def _():
-                    ar_wait(first + t, sem)
+                for ts in messages:
+                    if t == ts[0]:
+                        @pl.when(j > 0)
+                        def _():
+                            part = arbuf.at[pl.ds(first + t, len(ts))]
+                            pltpu.make_async_copy(part, part, sem.at[first + t]).wait()
 
             def recv_tile(j, t):
                 tile_waits(j, t, ar_rsem)
@@ -404,11 +416,7 @@
                     add_moments(z, t * TILE)
                 return 0
             lax.fori_loop(0, CHUNKS, down_body, 0)
-            for t in range(tiles):
-                pack_moments(ar_out + t, t * TILE)
-            every_tile = pl.ds(ar_out, tiles)
-            for k in peers:
-                remote(arsend.at[every_tile], arbuf.at[every_tile, k - 1], ar_ssem.at[ar_out], ar_rsem.at[ar_out], lax.rem(me + k, groups)).start()
+            send_tiles(ar_out, tuple(range(tiles)))
 
             def wait_d(c, _):
                 @pl.when(has_prev)
@@ -513,15 +521,18 @@
                     cols = slice(t * TILE, (t + 1) * TILE)
 
                     def out_body(c, _):
-                        rows_at = pl.ds(pl.multiple_of(c * (points // OUT_STEPS), points // OUT_STEPS), points // OUT_STEPS)
+                        rows_at = pl.ds(c * (points // OUT_STEPS), points // OUT_STEPS)
                         if t == 0:
                             u2[rows_at, :] = norm_relu(zb[rows_at, 0:chan_m], 0).astype(BF16)
                         z = dot(u2[rows_at, :], wout[j, :, cols])
                         zb[rows_at, cols] = z
                         add_moments(z, t * TILE)
                         return 0
-                    lax.fori_loop(0, OUT_STEPS, out_body, 0)
-                    send_moments(ar_out + (j + 1) * tiles + t, t * TILE)
+                    for c in range(OUT_STEPS):
+                        out_body(c, 0)
+                    for ts in messages:
+                        if t == ts[-1]:
+                            send_tiles(ar_out + (j + 1) * tiles, ts)
                     if t == 0:
                         @pl.when(j == blocks - 1)
                         def _():

time: 252 us -> 249 us (0.988)
  no operation moved by 1% of the time
where the time goes in v4:
time: 249 us
  Pallas kernels  249 us (100%)
    pallas_call x1, Pallas kernels, forward(): pl.pallas_call(kernel, out_shape=(jax.ShapeDtypeStruct((points, chan_b),...  239 us
    pallas_call x1, Pallas kernels, forward(): pl.pallas_call(finish, grid=(LAST_STEPS,), out_shape=jax.ShapeDtypeStruct...  9.7 us

profile of v4, /device:TPU:21, one launch (start us, length us, event | category | flops | bytes accessed | tf_op | source)
XLA Modules:
  0.0 249.2 jit_solution(9803821916150639401)
XLA Ops:
  0.0 239.5 %conv_stack.1 = (bf16[4096,1024]{1,0:T(8,128)(2,1)}, bf16[4096,256]{1,0:T(8,128)(2,1)}, f32[8,1024]{1,0:T(8,128)}) custom-call(bf16[32,2,256,128]{3,2,1,0:T(8,128)(2,1)} %images.1, bf16[2,3,3,128,128]{4,3,2,1,0:T(8,128)(2,1)} %w_a.1, bf16[3,3,128,1024]{3,2,1,0:T(8,128)(2,1)} %w_down.1, bf16[3,1024,256]{2,1,0:T(8,128)(2,1)} %w_in.1, ...), custom_call_target="tpu_custom_call" | custom-call | tf_op jit(solution)/shard_map/conv_stack/pallas_call | solution.py:591
  239.5 9.7 %last_norm.1 = bf16[4096,1024]{1,0:T(8,128)(2,1)} custom-call(bf16[4096,256]{1,0:T(8,128)(2,1)} %get-tuple-element.8.branch_ref, bf16[4096,1024]{1,0:T(8,128)(2,1)} %get-tuple-element.9.h_ref, bf16[3,256,1024]{2,1,0:T(8,128)(2,1)} %w_ref.1, f32[8,1024]{1,0:T(8,128)} %get-tuple-element.10.nrm_ref), custom_call_target="tpu_custom_call" | custom-call | tf_op jit(solution)/shard_map/last_norm/pallas_call | solution.py:613

commit v5 on v4

--- a/solution.py
+++ b/solution.py
@@ -10,7 +10,7 @@
 ROW_STEPS = 8
 IN_STEPS = 4
 OUT_STEPS = 2
-LAST_STEPS = 4
+LAST_STEPS = 2
 EARLY_A = 4
 EARLY_B = 4
 TILE = 256

time: 249 us -> 248 us (level)
  no operation moved by 1% of the time
where the time goes in v5:
time: 248 us
  Pallas kernels  248 us (100%)
    pallas_call x1, Pallas kernels, forward(): pl.pallas_call(kernel, out_shape=(jax.ShapeDtypeStruct((points, chan_b),...  239 us
    pallas_call x1, Pallas kernels, forward(): pl.pallas_call(finish, grid=(LAST_STEPS,), out_shape=jax.ShapeDtypeStruct...  8.54 us

profile of v5, /device:TPU:21, one launch (start us, length us, event | category | flops | bytes accessed | tf_op | source)
XLA Modules:
  0.0 248.0 jit_solution(735564787429641664)
XLA Ops:
  0.0 239.5 %conv_stack.1 = (bf16[4096,1024]{1,0:T(8,128)(2,1)}, bf16[4096,256]{1,0:T(8,128)(2,1)}, f32[8,1024]{1,0:T(8,128)}) custom-call(bf16[32,2,256,128]{3,2,1,0:T(8,128)(2,1)} %images.1, bf16[2,3,3,128,128]{4,3,2,1,0:T(8,128)(2,1)} %w_a.1, bf16[3,3,128,1024]{3,2,1,0:T(8,128)(2,1)} %w_down.1, bf16[3,1024,256]{2,1,0:T(8,128)(2,1)} %w_in.1, ...), custom_call_target="tpu_custom_call" | custom-call | tf_op jit(solution)/shard_map/conv_stack/pallas_call | solution.py:591
  239.5 8.5 %last_norm.1 = bf16[4096,1024]{1,0:T(8,128)(2,1)} custom-call(bf16[4096,256]{1,0:T(8,128)(2,1)} %get-tuple-element.8.branch_ref, bf16[4096,1024]{1,0:T(8,128)(2,1)} %get-tuple-element.9.h_ref, bf16[3,256,1024]{2,1,0:T(8,128)(2,1)} %w_ref.1, f32[8,1024]{1,0:T(8,128)} %get-tuple-element.10.nrm_ref), custom_call_target="tpu_custom_call" | custom-call | tf_op jit(solution)/shard_map/last_norm/pallas_call | solution.py:613
